TPU v7x, 32 devices: a whole 2x2x4 slice. The times are simulated.
32 devices in a mesh: dp: 4 (over y, x), vocab: 8 (over z, core).
Axes of the slice: x: 2, y: 2, z: 4, core: 2. Of those that a mesh axis runs over, the one named last changes fastest.
Arguments:
- hidden: bfloat16 [4, 32, 3584], P('dp', None, 'vocab'), may hold values from -6 to 6
- kl_hidden: bfloat16 [4, 32, 3584], P('dp', None, 'vocab'), may hold values from -6 to 6
- head_weight: bfloat16 [256000, 3584], P(('dp', 'vocab')), may hold values from -0.3125 to 0.3125
- labels: int32 [4, 32], P('dp'), may hold values from 0 to 255999
- token_mask: int32 [4, 32], P('dp'), may hold values 0 or 1
- kl_pair: int32 [4], P('dp'), may hold values from 0 to 3, as said below
- desirable: int32 [4], P('dp'), may hold values 0 or 1
- ref_logps: float32 [4, 64], P('dp', 'vocab'), may hold values from -23 to -11
Outputs:
- token_logps: float32 [4, 64], P('dp', 'vocab')
- seq_losses: float32 [4], P('dp')
- loss: float32 [], replicated
Inputs may be any that keep to these rules, and one draw needn't show every extreme that they name: kl_pair is a permutation of the 4 sequences with kl_pair[s] != s.
All inputs are finite; a program needn't handle non-finite values. No bound on the sum of `token_mask` or of `desirable` on one device may be relied on, other than what follows from the above.
Results may differ from a plain program's by a relative error of at most 0.0003.
Values may be sent and summed in bfloat16 or wider, within the bound.
A program may use at most 128 MiB of HBM per device.

v0:
```python
import jax
import jax.numpy as jnp
from jax import lax
from jax.sharding import PartitionSpec as P

kto_beta = 0.1
desirable_weight = 1.0
undesirable_weight = 1.33


def label_terms(logits, targets, first_row):
    shifted = targets - first_row
    inside = (shifted >= 0) & (shifted < logits.shape[1])
    clipped = jnp.clip(shifted, 0, logits.shape[1] - 1)
    picked = jnp.take_along_axis(logits, clipped[:, None], axis=1)[:, 0]
    return (jnp.sum(jnp.exp(logits), axis=1), jnp.where(inside, picked, 0.0))


def kto_losses(logratio, kl_total, seq_total, desirable):
    kl_estimate = kl_total / seq_total
    wanted = desirable_weight * (1.0 - jax.nn.sigmoid(kto_beta * (logratio - kl_estimate)))
    unwanted = undesirable_weight * (1.0 - jax.nn.sigmoid(kto_beta * (kl_estimate - logratio)))
    return jnp.where(desirable == 1, wanted, unwanted)


def on_device(hidden, kl_hidden, head_weight, labels, token_mask, kl_pair, desirable, ref_logps):
    sub_seq = hidden.shape[0]
    length = hidden.shape[1]
    vocab_rows = head_weight.shape[0]
    model_width = head_weight.shape[1]
    groups = lax.axis_size("vocab")
    vocab_index = lax.axis_index("vocab")
    data_index = lax.axis_index("dp")
    first_row = (data_index * groups + vocab_index) * vocab_rows
    all_labels, all_masks, all_pairs, all_desirable = (
        lax.all_gather(labels, "dp", axis=0, tiled=True),
        lax.all_gather(token_mask, "dp", axis=0, tiled=True),
        lax.all_gather(kl_pair, "dp", axis=0, tiled=True),
        lax.all_gather(desirable, "dp", axis=0, tiled=True),
    )
    targets = jnp.concatenate([all_labels, all_labels[all_pairs]], axis=1)
    weights_mask = jnp.concatenate([all_masks, all_masks[all_pairs]], axis=1).astype(jnp.float32)
    seq_total = targets.shape[0]
    columns = targets.shape[1]
    combined = jnp.concatenate([hidden, kl_hidden], axis=1)
    whole_rows = lax.all_gather(combined, "vocab", axis=2, tiled=True)
    portion = lax.all_gather(whole_rows, "dp", axis=0, tiled=True)
    number = portion.shape[0]
    logits = lax.dot_general(
        portion.reshape(number * columns, model_width),
        head_weight,
        (((1,), (1,)), ((), ())),
        preferred_element_type=jnp.float32,
    )
    portion_targets = targets.reshape(-1)
    part_sum, part_pick = label_terms(logits, portion_targets, first_row)
    token_stats = jnp.stack(
        [part_sum.reshape(number, columns), part_pick.reshape(number, columns)], axis=1
    )
    partition = token_stats[:, 0]
    picked = token_stats[:, 1]
    own_cols = columns // groups
    row_start = data_index * sub_seq
    col_start = vocab_index * own_cols
    ref_full = lax.dynamic_update_slice(
        jnp.zeros((seq_total, columns), jnp.float32), ref_logps, (row_start, col_start)
    )
    partition, picked, ref_all = lax.psum((partition, picked, ref_full), ("dp", "vocab"))
    token_logps = picked - jnp.log(partition)
    differences = weights_mask * (token_logps - ref_all)
    logratio = jnp.sum(differences[:, :length], axis=1)
    kl_terms = jnp.sum(differences[:, length:], axis=1)
    losses = kto_losses(logratio, jnp.sum(kl_terms), seq_total, all_desirable)
    own_logps = lax.dynamic_slice(token_logps, (row_start, col_start), (sub_seq, own_cols))
    own_losses = lax.dynamic_slice_in_dim(losses, row_start, sub_seq, 0)
    return (own_logps, own_losses, jnp.mean(losses))


def solution(mesh):
    in_specs = (
        P("dp", None, "vocab"),
        P("dp", None, "vocab"),
        P(("dp", "vocab"), None),
        P("dp", None),
        P("dp", None),
        P("dp"),
        P("dp"),
        P("dp", "vocab"),
    )
    out_specs = (P("dp", "vocab"), P("dp"), P())
    return jax.shard_map(
        on_device, mesh=mesh, in_specs=in_specs, out_specs=out_specs, check_vma=False
    )
```

profile of v0, /device:TPU:0, one launch (start us, length us, event | category | flops | bytes accessed | tf_op | source)
XLA Modules:
  0.0 153.6 jit_solution(2589287121122592298)
XLA Ops:
  7.2 0.0 all-gather.4.cloned.1.call-start
  7.2 0.8 pad_maximum_fusion
  8.0 0.2 copy.14
  8.2 23.7 %all_gather.20 = bf16[1,64,3584]{1,0,2:T(2,128)(2,1)S(1)} all-gather(bf16[1,64,448]{1,0,2:T(2,128)(2,1)S(1)} %copy.14), channel_id=1, replica_groups=mesh['dp'=4,'vocab'=8] {'vocab'}, dimensions={2}, use_global_device_ids=true | all-gather | bytes 516096 | tf_op jit(solution)/shard_map/all_gather | solution.py:46
  31.8 3.1 %copy.15 = bf16[1,64,3584]{2,1,0:T(8,128)(2,1)} copy(bf16[1,64,3584]{1,0,2:T(2,128)(2,1)S(1)} %all_gather.20) | data formatting | bytes 917504 | tf_op jit(solution)/shard_map/all_gather | solution.py:46
  34.9 0.0 all-gather.4.cloned.1.call-update
  36.2 1.2 dynamic-slice
  37.5 0.8 dynamic-update-slice
  38.3 0.8 dynamic-update-slice.1
  39.0 7.4 %all-reduce.2 = (s32[4]{0:T(128)S(1)}, s32[4]{0:T(128)S(1)}) all-reduce(s32[4]{0:T(128)S(1)} %dynamic-update-slice, s32[4]{0:T(128)S(1)} %dynamic-update-slice.1), channel_id=1, replica_groups=mesh['dp'=4,'vocab'=8] {'dp'}, use_global_device_ids=true, to_apply=%add | all-reduce | flops 8 | bytes 64
  46.4 7.9 %all-gather.1 = s32[4,1,32]{2,1,0:T(1,128)S(1)} all-gather(s32[1,1,32]{2,1,0:T(1,128)} %bitcast.17), channel_id=1, replica_groups=mesh['dp'=4,'vocab'=8] {'dp'}, dimensions={0}, use_global_device_ids=true | all-gather | bytes 640 | tf_op jit(solution)/shard_map/all_gather | solution.py:37
  54.3 0.6 gather_fusion.1
  54.9 7.2 %all-gather = s32[4,1,32]{2,1,0:T(1,128)S(1)} all-gather(s32[1,1,32]{2,1,0:T(1,128)} %bitcast.18), channel_id=1, replica_groups=mesh['dp'=4,'vocab'=8] {'dp'}, dimensions={0}, use_global_device_ids=true | all-gather | bytes 640 | tf_op jit(solution)/shard_map/all_gather | solution.py:36
  62.1 0.6 gather_fusion
  62.7 0.1 broadcast_clamp_fusion
  62.8 0.1 min.12
  62.8 0.8 dynamic_update_slice.3
  63.7 4.1 %all-gather.4.cloned.1.call-done = bf16[4,64,3584]{2,1,0:T(8,128)(2,1)} async-done(((bf16[1,64,3584]{2,1,0:T(8,128)(2,1)}), bf16[4,64,3584]{2,1,0:T(8,128)(2,1)}) %all-gather.4.cloned.1.call-update) | async-done | bytes 1835024 | tf_op jit(solution)/shard_map/all_gather | solution.py:47
  67.7 25.9 %exponential_reduce_fusion = (f32[256]{0:T(256)S(1)}, f32[256,8000]{0,1:T(8,128)}) fusion(bf16[256,3584]{1,0:T(8,128)(2,1)} %bitcast.19, bf16[8000,3584]{1,0:T(8,128)(2,1)} %param.10), kind=kOutput, calls=%fused_computation.3 | convolution fusion | flops 14682112000 | bytes 67372032 | tf_op jit(solution)/shard_map/dot_general | solution.py:49
  93.6 9.0 %gather_fusion.2 = f32[256]{0:T(256)S(1)} fusion(f32[256,8000]{0,1:T(8,128)} %get-tuple-element.15, s32[256]{0:T(256)S(1)} %bitcast.11), kind=kCustom, calls=%fused_computation.2 | custom fusion | bytes 4096 | tf_op jit(solution)/shard_map/jit(take_along_axis)/gather | solution.py:15
  102.6 0.1 gather.14
  102.7 0.1 select_select_fusion
  102.7 0.1 squeeze_stack_reshape.4
  102.8 38.9 %all-reduce.3 = (f32[4,64]{1,0:T(4,128)S(1)}, f32[4,64]{1,0:T(4,128)S(1)}, f32[4,64]{1,0:T(4,128)S(1)}) all-reduce(f32[4,64]{1,0:T(4,128)S(1)} %select_select_fusion, f32[4,64]{1,0:T(4,128)S(1)} %squeeze_stack_reshape.4, f32[4,64]{1,0:T(4,128)S(1)} %dynamic_update_slice.3), channel_id=1, replica_groups=mesh['dp'=4,'vocab'=8] {'dp','vocab'}, use_global_device_ids=true, to_apply=%region_0.1 | all-reduce | flops 768 | bytes 6144 | tf_op jit(solution)/shard_map/psum | solution.py:68
  141.8 0.1 fusion
  141.8 0.6 dynamic_slice.6
  142.4 0.7 slice_reduce_fusion
  143.7 0.6 fusion.4
  144.4 0.6 dynamic_slice.7
  (9 shorter events, 0.0 us)
Async XLA Ops:
  7.2 60.6 %all-gather.4.cloned.1.call-start = ((), (), s32[]{:S(2)}) async-start(), calls=%async_computation | async-start | bytes 2293760 | tf_op jit(solution)/shard_map/all_gather | solution.py:47
Sparse Core Ops, SparseCore 0:
  35.1 32.6 all-gather.3
where the time goes:
time: 154 us
  blocking collectives  85.1 us (55%)
  matrix products  25.9 us (17%)
  local copies, waits for them, and re-layouts  18.3 us (12%)
  between operations  17.8 us (12%)
  waiting for transfers between devices  4.07 us (3%)
  other arithmetic  2.34 us (2%)
    psum x1, blocking collectives, on_device(): lax.psum((partition, picked, ref_full), ('dp', 'vocab'))  38.9 us
    dot_general x1, matrix products, on_device(): lax.dot_general(portion.reshape(number * columns, model_width), head_weig...  25.9 us
    all_gather x1, blocking collectives, on_device(): whole_rows = lax.all_gather(combined, 'vocab', axis=2, tiled=True)  23.7 us
    gather x2, local copies, waits for them, and re-layouts, label_terms(): picked = jnp.take_along_axis(logits, clipped[:, None], axis=1)[:, 0]  9.07 us
    all_gather x1, blocking collectives, on_device(): lax.all_gather(token_mask, 'dp', axis=0, tiled=True)  7.92 us
    unnamed x1, blocking collectives  7.39 us
    all_gather x1, blocking collectives, on_device(): lax.all_gather(labels, 'dp', axis=0, tiled=True)  7.23 us
    all_gather x1, waiting for transfers between devices, on_device(): portion = lax.all_gather(whole_rows, 'dp', axis=0, tiled=True)  4.05 us
  transfers between devices with their start and end apart: 1, of which 1 were waited for; matrix products, arithmetic and copies ran while one was open for 3% of the time, Pallas kernels for 0%

commit v1 on v0

--- a/solution.py
+++ b/solution.py
@@ -6,6 +6,7 @@
 kto_beta = 0.1
 desirable_weight = 1.0
 undesirable_weight = 1.33
+wait_the_panels = lambda mine: lax.psum(lax.psum(mine, axis_name="vocab"), axis_name="dp")
 
 
 def label_terms(logits, targets, first_row):
@@ -65,7 +66,7 @@
     ref_full = lax.dynamic_update_slice(
         jnp.zeros((seq_total, columns), jnp.float32), ref_logps, (row_start, col_start)
     )
-    partition, picked, ref_all = lax.psum((partition, picked, ref_full), ("dp", "vocab"))
+    partition, picked, ref_all = wait_the_panels((partition, picked, ref_full))
     token_logps = picked - jnp.log(partition)
     differences = weights_mask * (token_logps - ref_all)
     logratio = jnp.sum(differences[:, :length], axis=1)

time: 154 us -> 141 us (0.916)
  blocking collectives: 85.1 us -> 71.9 us
    psum x1 -> x2, blocking collectives: 38.9 us -> 25.7 us  [the longest x1 15.1 us: lax.psum(mine, axis_name='vocab')]
where the time goes in v1:
time: 141 us; the launch traced here: 140 us
  blocking collectives  71.9 us (51%)
  matrix products  25.9 us (18%)
  local copies, waits for them, and re-layouts  18.3 us (13%)
  between operations  17.8 us (13%)
  waiting for transfers between devices  4.07 us (3%)
  other arithmetic  2.35 us (2%)
    dot_general x1, matrix products, on_device(): lax.dot_general(portion.reshape(number * columns, model_width), head_weig...  25.9 us
    all_gather x1, blocking collectives, on_device(): whole_rows = lax.all_gather(combined, 'vocab', axis=2, tiled=True)  23.7 us
    psum x1, blocking collectives, lax.psum(mine, axis_name='vocab')  15.1 us
    psum x1, blocking collectives, lax.psum(lax.psum(mine, axis_name='vocab'), axis_name='dp')  10.6 us
    gather x2, local copies, waits for them, and re-layouts, label_terms(): picked = jnp.take_along_axis(logits, clipped[:, None], axis=1)[:, 0]  9.07 us
    all_gather x1, blocking collectives, on_device(): lax.all_gather(token_mask, 'dp', axis=0, tiled=True)  7.92 us
    unnamed x1, blocking collectives  7.39 us
    all_gather x1, blocking collectives, on_device(): lax.all_gather(labels, 'dp', axis=0, tiled=True)  7.23 us
  transfers between devices with their start and end apart: 1, of which 1 were waited for; matrix products, arithmetic and copies ran while one was open for 3% of the time, Pallas kernels for 0%

profile of v1, /device:TPU:0, one launch (start us, length us, event | category | flops | bytes accessed | tf_op | source)
XLA Modules:
  0.0 140.3 jit_solution(2754930158683218777)
XLA Ops:
  7.2 0.0 all-gather.4.cloned.1.call-start
  7.2 0.8 pad_maximum_fusion
  8.0 0.2 copy.14
  8.2 23.7 %all_gather.20 = bf16[1,64,3584]{1,0,2:T(2,128)(2,1)S(1)} all-gather(bf16[1,64,448]{1,0,2:T(2,128)(2,1)S(1)} %copy.14), channel_id=1, replica_groups=mesh['dp'=4,'vocab'=8] {'vocab'}, dimensions={2}, use_global_device_ids=true | all-gather | bytes 516096 | tf_op jit(solution)/shard_map/all_gather | solution.py:47
  31.8 3.1 %copy.15 = bf16[1,64,3584]{2,1,0:T(8,128)(2,1)} copy(bf16[1,64,3584]{1,0,2:T(2,128)(2,1)S(1)} %all_gather.20) | data formatting | bytes 917504 | tf_op jit(solution)/shard_map/all_gather | solution.py:47
  34.9 0.0 all-gather.4.cloned.1.call-update
  36.2 1.2 dynamic-slice
  37.5 0.8 dynamic-update-slice
  38.3 0.8 dynamic-update-slice.1
  39.0 7.4 %all-reduce.2 = (s32[4]{0:T(128)S(1)}, s32[4]{0:T(128)S(1)}) all-reduce(s32[4]{0:T(128)S(1)} %dynamic-update-slice, s32[4]{0:T(128)S(1)} %dynamic-update-slice.1), channel_id=1, replica_groups=mesh['dp'=4,'vocab'=8] {'dp'}, use_global_device_ids=true, to_apply=%add | all-reduce | flops 8 | bytes 64
  46.4 7.9 %all-gather.1 = s32[4,1,32]{2,1,0:T(1,128)S(1)} all-gather(s32[1,1,32]{2,1,0:T(1,128)} %bitcast.17), channel_id=1, replica_groups=mesh['dp'=4,'vocab'=8] {'dp'}, dimensions={0}, use_global_device_ids=true | all-gather | bytes 640 | tf_op jit(solution)/shard_map/all_gather | solution.py:38
  54.3 0.6 gather_fusion.1
  54.9 7.2 %all-gather = s32[4,1,32]{2,1,0:T(1,128)S(1)} all-gather(s32[1,1,32]{2,1,0:T(1,128)} %bitcast.18), channel_id=1, replica_groups=mesh['dp'=4,'vocab'=8] {'dp'}, dimensions={0}, use_global_device_ids=true | all-gather | bytes 640 | tf_op jit(solution)/shard_map/all_gather | solution.py:37
  62.1 0.6 gather_fusion
  62.7 0.1 broadcast_clamp_fusion
  62.8 0.1 min.12
  62.8 0.8 dynamic_update_slice.3
  63.7 4.1 %all-gather.4.cloned.1.call-done = bf16[4,64,3584]{2,1,0:T(8,128)(2,1)} async-done(((bf16[1,64,3584]{2,1,0:T(8,128)(2,1)}), bf16[4,64,3584]{2,1,0:T(8,128)(2,1)}) %all-gather.4.cloned.1.call-update) | async-done | bytes 1835024 | tf_op jit(solution)/shard_map/all_gather | solution.py:48
  67.7 25.9 %exponential_reduce_fusion = (f32[256]{0:T(256)S(1)}, f32[256,8000]{0,1:T(8,128)}) fusion(bf16[256,3584]{1,0:T(8,128)(2,1)} %bitcast.19, bf16[8000,3584]{1,0:T(8,128)(2,1)} %param.10), kind=kOutput, calls=%fused_computation.3 | convolution fusion | flops 14682112000 | bytes 67372032 | tf_op jit(solution)/shard_map/dot_general | solution.py:50
  93.6 9.0 %gather_fusion.2 = f32[256]{0:T(256)S(1)} fusion(f32[256,8000]{0,1:T(8,128)} %get-tuple-element.18, s32[256]{0:T(256)S(1)} %bitcast.11), kind=kCustom, calls=%fused_computation.2 | custom fusion | bytes 4096 | tf_op jit(solution)/shard_map/jit(take_along_axis)/gather | solution.py:16
  102.6 0.1 gather.14
  102.7 0.1 select_select_fusion
  102.7 0.1 squeeze_stack_reshape.4
  102.8 15.1 %all-reduce.3 = (f32[4,64]{1,0:T(4,128)S(1)}, f32[4,64]{1,0:T(4,128)S(1)}, f32[4,64]{1,0:T(4,128)S(1)}) all-reduce(f32[4,64]{1,0:T(4,128)S(1)} %select_select_fusion, f32[4,64]{1,0:T(4,128)S(1)} %squeeze_stack_reshape.4, f32[4,64]{1,0:T(4,128)S(1)} %dynamic_update_slice.3), channel_id=1, replica_groups=mesh['dp'=4,'vocab'=8] {'vocab'}, use_global_device_ids=true, to_apply=%region_0.1 | all-reduce | flops 768 | bytes 6144 | tf_op jit(solution)/shard_map/psum | solution.py:9
  117.9 10.6 %all-reduce.4 = (f32[4,64]{1,0:T(4,128)S(1)}, f32[4,64]{1,0:T(4,128)S(1)}, f32[4,64]{1,0:T(4,128)S(1)}) all-reduce(f32[4,64]{1,0:T(4,128)S(1)} %get-tuple-element.7, f32[4,64]{1,0:T(4,128)S(1)} %get-tuple-element.8, f32[4,64]{1,0:T(4,128)S(1)} %get-tuple-element.9), channel_id=1, replica_groups=mesh['dp'=4,'vocab'=8] {'dp'}, use_global_device_ids=true, to_apply=%region_1.2 | all-reduce | flops 768 | bytes 6144 | tf_op jit(solution)/shard_map/psum | solution.py:9
  128.5 0.1 fusion
  128.6 0.6 dynamic_slice.6
  129.2 0.7 slice_reduce_fusion
  130.5 0.6 fusion.4
  131.1 0.6 dynamic_slice.7
  (9 shorter events, 0.0 us)
Async XLA Ops:
  7.2 60.6 %all-gather.4.cloned.1.call-start = ((), (), s32[]{:S(2)}) async-start(), calls=%async_computation | async-start | bytes 2293760 | tf_op jit(solution)/shard_map/all_gather | solution.py:48
Sparse Core Ops, SparseCore 0:
  35.1 32.6 all-gather.3
